TPU v7x, 32 devices: a whole 2x2x4 slice. The times are simulated.
32 devices in a mesh: row: 8 (over z, y), col: 4 (over x, core).
Axes of the slice: x: 2, y: 2, z: 4, core: 2. Of those that a mesh axis runs over, the one named last changes fastest.
Arguments:
- act_quant: bfloat16 [512, 8192], P('row', 'col'), may hold values from -127 to 127, as said below
- act_scale: float32 [512], replicated, may hold values from 0.004 to 0.04
- gate_up_quant: bfloat16 [2, 8192, 29568], P(None, 'col', 'row'), may hold values from -127 to 127, as said below
- gate_up_scale: float32 [2, 29568], P(None, 'row'), may hold values from 5e-05 to 0.0005
- down_quant: bfloat16 [29568, 8192], P('row', 'col'), may hold values from -127 to 127, as said below
- down_scale: float32 [8192], P('col'), may hold values from 3e-05 to 0.0003
Outputs:
- mixed_out: bfloat16 [512, 8192], P('row', 'col')
Inputs may be any that keep to these rules, and one draw needn't show every extreme that they name: `act_quant`: whole numbers. `gate_up_quant`: whole numbers. `down_quant`: whole numbers.
All inputs are finite; a program needn't handle non-finite values.
Results may differ from a plain program's by a relative error of at most 0.005.
Values may be sent and summed in bfloat16 or wider, within the bound.
A program may use at most 128 MiB of HBM per device.

v0:
```python
import jax
import jax.numpy as jnp
from jax import lax
from jax.sharding import PartitionSpec as P


def body(act_quant, act_scale, gate_up_quant, gate_up_scale, down_quant, down_scale):
    feature_width = gate_up_quant.shape[2]
    gathered = lax.all_gather(act_quant, "row", axis=0, tiled=True)
    share_rows = gathered.shape[0] // lax.axis_size("col")
    gate_part = jnp.dot(gathered, gate_up_quant[0], preferred_element_type=jnp.float32)
    up_part = jnp.dot(gathered, gate_up_quant[1], preferred_element_type=jnp.float32)
    summed = lax.psum_scatter(
        jnp.concatenate([gate_part, up_part], axis=1), "col", scatter_dimension=0, tiled=True
    )
    token_scale = lax.dynamic_slice_in_dim(
        act_scale, lax.axis_index("col") * share_rows, share_rows, 0
    )
    gate_val = summed[:, :feature_width] * token_scale[:, None] * gate_up_scale[0][None, :]
    up_val = summed[:, feature_width:] * token_scale[:, None] * gate_up_scale[1][None, :]
    hidden = (jax.nn.silu(gate_val) * up_val).astype(jnp.bfloat16)
    hidden = lax.all_gather(hidden, "col", axis=0, tiled=True)
    mixed_out = lax.psum_scatter(
        jnp.dot(hidden, down_quant, preferred_element_type=jnp.float32) * down_scale[None, :],
        "row",
        scatter_dimension=0,
        tiled=True,
    )
    return mixed_out.astype(jnp.bfloat16)


def solution(mesh):
    in_specs = (
        P("row", "col"),
        P(),
        P(None, "col", "row"),
        P(None, "row"),
        P("row", "col"),
        P("col"),
    )
    out_specs = P("row", "col")
    return jax.shard_map(body, mesh=mesh, in_specs=in_specs, out_specs=out_specs, check_vma=False)
```

profile of v0, /device:TPU:0, one launch (start us, length us, event | category | flops | bytes accessed | tf_op | source)
XLA Modules:
  0.0 351.1 jit_solution(16619677064941690027)
XLA Ops:
  6.5 0.0 all-gather.3.cloned.1.call-start
  6.5 0.7 all-gather.3.cloned.1.call-update
  7.3 0.0 reduce-scatter.3.cloned.1.call-start
  7.3 54.0 %all-gather.3.cloned.1.call-done = bf16[512,2048]{1,0:T(8,128)(2,1)} async-done(((bf16[64,2048]{1,0:T(8,128)(2,1)}), bf16[512,2048]{1,0:T(8,128)(2,1)}) %all-gather.3.cloned.1.call-update) | async-done | bytes 2097168 | tf_op jit(solution)/shard_map/all_gather | solution.py:9
  61.3 11.8 %fusion = f32[512,3696]{0,1:T(8,128)S(1)} fusion(bf16[512,2048]{1,0:T(8,128)(2,1)} %all-gather.3.cloned.1.call-done, bf16[2,2048,3696]{1,2,0:T(8,128)(2,1)} %param.8), kind=kOutput, calls=%fused_computation.1 | convolution fusion | flops 7751073792 | bytes 24805376 | tf_op jit(solution)/shard_map/dot_general | solution.py:12
  73.1 11.8 %fusion.2 = f32[512,3696]{0,1:T(8,128)S(1)} fusion(bf16[512,2048]{1,0:T(8,128)(2,1)} %all-gather.3.cloned.1.call-done, bf16[2,2048,3696]{1,2,0:T(8,128)(2,1)} %param.8), kind=kOutput, calls=%fused_computation.3 | convolution fusion | flops 7751073792 | bytes 24805376 | tf_op jit(solution)/shard_map/dot_general | solution.py:11
  84.9 6.2 %pad_maximum_fusion = f32[512,7392]{0,1:T(8,128)} fusion(f32[512,3696]{0,1:T(8,128)S(1)} %fusion, f32[512,3696]{0,1:T(8,128)S(1)} %fusion.2), kind=kLoop, calls=%fused_computation | loop fusion | flops 3784704 | bytes 30277632 | tf_op jit(solution)/shard_map/concatenate | solution.py:14
  91.2 0.0 copy-start
  91.2 0.0 reduce-scatter.3.cloned.1.call-update
  91.2 0.0 copy-start.1
  91.2 0.0 all-gather.5.cloned.1.call-start
  91.3 0.8 dynamic_slice.3
  92.0 0.0 copy-done
  92.0 0.1 slice_reduce_fusion.1
  92.1 110.6 %reduce-scatter.3.cloned.1.call-done = f32[128,7392]{0,1:T(8,128)} async-done(((f32[512,7392]{0,1:T(8,128)}), f32[128,7392]{0,1:T(8,128)}) %reduce-scatter.3.cloned.1.call-update) | async-done | bytes 3784720 | tf_op jit(solution)/shard_map/reduce_scatter | solution.py:13
  202.7 4.8 %fusion.8 = bf16[128,3696]{0,1:T(8,128)(2,1)} fusion(f32[128,7392]{0,1:T(8,128)} %reduce-scatter.3.cloned.1.call-done, f32[3696]{0:T(1024)S(1)} %get-tuple-element.6, f32[3696]{0:T(1024)S(1)} %get-tuple-element.5, f32[128]{0:T(128)S(1)} %dynamic_slice.3), kind=kLoop, calls=%fused_computation.11 | loop fusion | flops 4730880 | bytes 4760960 | tf_op jit(solution)/shard_map/convert_element_type | solution.py:21
  207.5 0.0 all-gather.5.cloned.1.call-update
  207.5 0.0 reduce-scatter.5.cloned.1.call-start
  207.6 32.7 %all-gather.5.cloned.1.call-done = bf16[512,3696]{0,1:T(8,128)(2,1)} async-done(((bf16[128,3696]{0,1:T(8,128)(2,1)}), bf16[512,3696]{0,1:T(8,128)(2,1)}) %all-gather.5.cloned.1.call-update) | async-done | bytes 3784720 | tf_op jit(solution)/shard_map/all_gather | solution.py:22
  240.3 0.0 copy-done.1
  240.3 14.1 %convolution_multiply_fusion = f32[512,2048]{1,0:T(8,128)} fusion(bf16[512,3696]{0,1:T(8,128)(2,1)} %all-gather.5.cloned.1.call-done, bf16[3696,2048]{1,0:T(8,128)(2,1)} %param.10, f32[2048]{0:T(1024)S(1)} %copy-done.1), kind=kOutput, calls=%fused_computation.7 | convolution fusion | flops 7752122368 | bytes 23126016 | tf_op jit(solution)/shard_map/dot_general | solution.py:24
  254.4 0.0 reduce-scatter.5.cloned.1.call-update
  254.4 88.4 %reduce-scatter.5.cloned.1.call-done = f32[64,2048]{1,0:T(8,128)} async-done(((f32[512,2048]{1,0:T(8,128)}), f32[64,2048]{1,0:T(8,128)}) %reduce-scatter.5.cloned.1.call-update) | async-done | bytes 524304 | tf_op jit(solution)/shard_map/reduce_scatter | solution.py:23
  342.8 1.8 convert_element_type.7
Async XLA Ops:
  6.5 54.8 %all-gather.3.cloned.1.call-start = ((), (), s32[]{:S(2)}) async-start(), calls=%async_computation.2 | async-start | bytes 2359296 | tf_op jit(solution)/shard_map/all_gather | solution.py:9
  7.3 195.5 %reduce-scatter.3.cloned.1.call-start = ((), (), s32[]{:S(2)}) async-start(), calls=%async_computation.3 | async-start | bytes 18923520 | tf_op jit(solution)/shard_map/reduce_scatter | solution.py:13
  91.2 0.9 copy-start
  91.2 149.1 %copy-start.1 = (f32[2048]{0:T(1024)S(1)}, f32[2048]{0:T(1024)}, u32[]{:S(2)}) copy-start(f32[2048]{0:T(1024)} %param.11) | copy-start | bytes 24580
  91.2 149.1 %all-gather.5.cloned.1.call-start = ((), (), s32[]{:S(2)}) async-start(), calls=%async_computation.4 | async-start | bytes 4730880 | tf_op jit(solution)/shard_map/all_gather | solution.py:22
  207.5 135.3 %reduce-scatter.5.cloned.1.call-start = ((), (), s32[]{:S(2)}) async-start(), calls=%async_computation.5 | async-start | bytes 4718592 | tf_op jit(solution)/shard_map/reduce_scatter | solution.py:23
Sparse Core Ops, SparseCore 0:
  9.5 51.7 all-gather.2
  91.3 111.3 reduce-scatter.2
  207.7 32.6 all-gather.4
  254.5 88.2 reduce-scatter.4
where the time goes:
time: 351 us
  waiting for transfers between devices  287 us (82%)
  matrix products  37.7 us (11%)
  between operations  13.2 us (4%)
  other arithmetic  12.8 us (4%)
    reduce_scatter x1, waiting for transfers between devices, body(): lax.psum_scatter(jnp.concatenate([gate_part, up_part], axis=1), 'col', sc...  111 us
    reduce_scatter x1, waiting for transfers between devices, body(): lax.psum_scatter(jnp.dot(hidden, down_quant, preferred_element_type=jnp.f...  88.4 us
    all_gather x1, waiting for transfers between devices, body(): gathered = lax.all_gather(act_quant, 'row', axis=0, tiled=True)  54 us
    all_gather x1, waiting for transfers between devices, body(): hidden = lax.all_gather(hidden, 'col', axis=0, tiled=True)  32.7 us
    dot_general x1, matrix products, body(): jnp.dot(hidden, down_quant, preferred_element_type=jnp.float32)  14.1 us
    dot_general x1, matrix products, body(): jnp.dot(gathered, gate_up_quant[0], preferred_element_type=jnp.float32)  11.8 us
    dot_general x1, matrix products, body(): jnp.dot(gathered, gate_up_quant[1], preferred_element_type=jnp.float32)  11.8 us
  transfers between devices with their start and end apart: 4, of which 4 were waited for; matrix products, arithmetic and copies ran while one was open for 0% of the time, Pallas kernels for 0%

commit v1 on v0

--- a/solution.py
+++ b/solution.py
@@ -6,7 +6,12 @@
 
 def body(act_quant, act_scale, gate_up_quant, gate_up_scale, down_quant, down_scale):
     feature_width = gate_up_quant.shape[2]
-    gathered = lax.all_gather(act_quant, "row", axis=0, tiled=True)
+    ring = [act_quant]
+    for hop in range(7):
+        ring.append(lax.ppermute(ring[-1], "row", [(dev, (dev + 1) % 8) for dev in range(8)]))
+    gathered = jnp.roll(
+        jnp.concatenate(ring[::-1], axis=0), (lax.axis_index("row") + 1) * ring[0].shape[0], axis=0
+    )
     share_rows = gathered.shape[0] // lax.axis_size("col")
     gate_part = jnp.dot(gathered, gate_up_quant[0], preferred_element_type=jnp.float32)
     up_part = jnp.dot(gathered, gate_up_quant[1], preferred_element_type=jnp.float32)

time: 351 us -> 382 us (1.088)
  local copies, waits for them, and re-layouts: 0.85 us -> 13.3 us
  waiting for transfers between devices: 287 us -> 296 us
    ppermute x0 -> x7, waiting for transfers between devices: none -> 66 us  [body(): lax.ppermute(ring[-1], 'row', [(dev, (dev + 1) % 8) for dev in range(8)])]
    all_gather x1 -> x0, waiting for transfers between devices: 54 us -> none  [body(): gathered = lax.all_gather(act_quant, 'row', axis=0, tiled=True)]
    unnamed x4 -> x21, local copies, waits for them, and re-layouts: 0.01 us -> 11.8 us
  transfers between devices with their start and end apart: 4 -> 10, of which waited for: 4 -> 10; matrix products, arithmetic and copies ran while one was open for 0% -> 0% of each run, Pallas kernels for 0% -> 0%
where the time goes in v1:
time: 382 us
  waiting for transfers between devices  296 us (77%)
  matrix products  39.7 us (10%)
  other arithmetic  15.9 us (4%)
  local copies, waits for them, and re-layouts  13.3 us (3%)
  between operations  13.2 us (3%)
    reduce_scatter x1, waiting for transfers between devices, body(): lax.psum_scatter(jnp.concatenate([gate_part, up_part], axis=1), 'col', sc...  109 us
    reduce_scatter x1, waiting for transfers between devices, body(): lax.psum_scatter(jnp.dot(hidden, down_quant, preferred_element_type=jnp.f...  88.5 us
    ppermute x7, waiting for transfers between devices, body(): lax.ppermute(ring[-1], 'row', [(dev, (dev + 1) % 8) for dev in range(8)])  66 us
    all_gather x1, waiting for transfers between devices, body(): hidden = lax.all_gather(hidden, 'col', axis=0, tiled=True)  32.5 us
    dot_general x1, matrix products, body(): jnp.dot(hidden, down_quant, preferred_element_type=jnp.float32)  14.1 us
    dot_general x1, matrix products, body(): jnp.dot(gathered, gate_up_quant[1], preferred_element_type=jnp.float32)  14 us
    unnamed x21, local copies, waits for them, and re-layouts  11.8 us
    dot_general x1, matrix products, body(): jnp.dot(gathered, gate_up_quant[0], preferred_element_type=jnp.float32)  11.6 us
  transfers between devices with their start and end apart: 10, of which 10 were waited for; matrix products, arithmetic and copies ran while one was open for 0% of the time, Pallas kernels for 0%

profile of v1, /device:TPU:0, one launch (start us, length us, event | category | flops | bytes accessed | tf_op | source)
XLA Modules:
  0.0 381.7 jit_solution(9686658294118683427)
XLA Ops:
  6.5 3.0 collective-permute-start
  9.5 9.6 %collective-permute-done = bf16[64,2048]{1,0:T(8,128)(2,1)S(1)} collective-permute-done((bf16[64,2048]{1,0:T(8,128)(2,1)}, bf16[64,2048]{1,0:T(8,128)(2,1)S(1)}, u32[]{:S(2)}, u32[]{:S(2)}) %collective-permute-start) | collective-permute-done | bytes 262176 | tf_op jit(solution)/shard_map/ppermute | solution.py:11
  19.2 10.2 %collective-permute-done.1 = bf16[64,2048]{1,0:T(8,128)(2,1)S(1)} collective-permute-done((bf16[64,2048]{1,0:T(8,128)(2,1)S(1)}, bf16[64,2048]{1,0:T(8,128)(2,1)S(1)}, u32[]{:S(2)}, u32[]{:S(2)}) %collective-permute-start.1) | collective-permute-done | bytes 262176 | tf_op jit(solution)/shard_map/ppermute | solution.py:11
  29.3 9.3 %collective-permute-done.2 = bf16[64,2048]{1,0:T(8,128)(2,1)S(1)} collective-permute-done((bf16[64,2048]{1,0:T(8,128)(2,1)S(1)}, bf16[64,2048]{1,0:T(8,128)(2,1)S(1)}, u32[]{:S(2)}, u32[]{:S(2)}) %collective-permute-start.2) | collective-permute-done | bytes 262176 | tf_op jit(solution)/shard_map/ppermute | solution.py:11
  38.6 9.1 %collective-permute-done.3 = bf16[64,2048]{1,0:T(8,128)(2,1)S(1)} collective-permute-done((bf16[64,2048]{1,0:T(8,128)(2,1)S(1)}, bf16[64,2048]{1,0:T(8,128)(2,1)S(1)}, u32[]{:S(2)}, u32[]{:S(2)}) %collective-permute-start.3) | collective-permute-done | bytes 262176 | tf_op jit(solution)/shard_map/ppermute | solution.py:11
  47.7 9.1 %collective-permute-done.4 = bf16[64,2048]{1,0:T(8,128)(2,1)S(1)} collective-permute-done((bf16[64,2048]{1,0:T(8,128)(2,1)S(1)}, bf16[64,2048]{1,0:T(8,128)(2,1)S(1)}, u32[]{:S(2)}, u32[]{:S(2)}) %collective-permute-start.4) | collective-permute-done | bytes 262176 | tf_op jit(solution)/shard_map/ppermute | solution.py:11
  56.8 9.7 %collective-permute-done.5 = bf16[64,2048]{1,0:T(8,128)(2,1)S(1)} collective-permute-done((bf16[64,2048]{1,0:T(8,128)(2,1)S(1)}, bf16[64,2048]{1,0:T(8,128)(2,1)S(1)}, u32[]{:S(2)}, u32[]{:S(2)}) %collective-permute-start.5) | collective-permute-done | bytes 262176 | tf_op jit(solution)/shard_map/ppermute | solution.py:11
  66.5 9.1 %collective-permute-done.6 = bf16[64,2048]{1,0:T(8,128)(2,1)S(1)} collective-permute-done((bf16[64,2048]{1,0:T(8,128)(2,1)S(1)}, bf16[64,2048]{1,0:T(8,128)(2,1)S(1)}, u32[]{:S(2)}, u32[]{:S(2)}) %collective-permute-start.6) | collective-permute-done | bytes 262176 | tf_op jit(solution)/shard_map/ppermute | solution.py:11
  76.2 0.7 constant_dynamic-update-slice_fusion.14
  77.0 0.7 constant_dynamic-update-slice_fusion.13
  78.4 0.7 constant_dynamic-update-slice_fusion.11
  80.6 1.7 constant_dynamic-update-slice_fusion.8
  84.4 0.7 constant_dynamic-update-slice_fusion.4
  85.1 0.7 constant_dynamic-update-slice_fusion.3
  88.0 11.6 %fusion.2 = f32[512,3696]{0,1:T(8,128)S(1)} fusion(bf16[2,2048,3696]{1,2,0:T(8,128)(2,1)} %param.8, bf16[1024,2048]{1,0:T(8,128)(2,1)} %constant_dynamic-update-slice_fusion, s32[]{:T(128)S(6)} %select_n.17), kind=kOutput, calls=%fused_computation.3 | convolution fusion | flops 7751073792 | bytes 24805380 | tf_op jit(solution)/shard_map/dot_general | solution.py:16
  99.7 14.0 %fusion = f32[512,3696]{0,1:T(8,128)} fusion(bf16[2,2048,3696]{1,2,0:T(8,128)(2,1)} %param.8, bf16[1024,2048]{1,0:T(8,128)(2,1)} %constant_dynamic-update-slice_fusion, s32[]{:T(128)S(6)} %select_n.17), kind=kOutput, calls=%fused_computation.1 | convolution fusion | flops 7751073792 | bytes 24805380 | tf_op jit(solution)/shard_map/dot_general | solution.py:17
  113.6 9.4 %pad_maximum_fusion = f32[512,7392]{0,1:T(8,128)} fusion(f32[512,3696]{0,1:T(8,128)} %fusion, f32[512,3696]{0,1:T(8,128)S(1)} %fusion.2), kind=kLoop, calls=%fused_computation | loop fusion | flops 3784704 | bytes 30277632 | tf_op jit(solution)/shard_map/concatenate | solution.py:19
  123.1 0.8 dynamic_slice.8
  123.9 109.2 %reduce-scatter.3.cloned.1.call-done = f32[128,7392]{0,1:T(8,128)} async-done(((f32[512,7392]{0,1:T(8,128)}), f32[128,7392]{0,1:T(8,128)}) %reduce-scatter.3.cloned.1.call-update) | async-done | bytes 3784720 | tf_op jit(solution)/shard_map/reduce_scatter | solution.py:18
  233.1 4.8 %fusion.8 = bf16[128,3696]{0,1:T(8,128)(2,1)} fusion(f32[128,7392]{0,1:T(8,128)} %reduce-scatter.3.cloned.1.call-done, f32[3696]{0:T(1024)S(1)} %get-tuple-element.6, f32[3696]{0:T(1024)S(1)} %get-tuple-element.5, f32[128]{0:T(128)S(1)} %dynamic_slice.8), kind=kLoop, calls=%fused_computation.11 | loop fusion | flops 4730880 | bytes 4760960 | tf_op jit(solution)/shard_map/convert_element_type | solution.py:26
  238.2 32.5 %all-gather.2.cloned.1.call-done = bf16[512,3696]{0,1:T(8,128)(2,1)} async-done(((bf16[128,3696]{0,1:T(8,128)(2,1)}), bf16[512,3696]{0,1:T(8,128)(2,1)}) %all-gather.2.cloned.1.call-update) | async-done | bytes 3784720 | tf_op jit(solution)/shard_map/all_gather | solution.py:27
  270.7 14.1 %convolution_multiply_fusion = f32[512,2048]{1,0:T(8,128)} fusion(bf16[512,3696]{0,1:T(8,128)(2,1)} %all-gather.2.cloned.1.call-done, bf16[3696,2048]{1,0:T(8,128)(2,1)} %param.10, f32[2048]{0:T(1024)S(1)} %copy-done.2), kind=kOutput, calls=%fused_computation.7 | convolution fusion | flops 7752122368 | bytes 23126016 | tf_op jit(solution)/shard_map/dot_general | solution.py:29
  284.9 88.5 %reduce-scatter.5.cloned.1.call-done = f32[64,2048]{1,0:T(8,128)} async-done(((f32[512,2048]{1,0:T(8,128)}), f32[64,2048]{1,0:T(8,128)}) %reduce-scatter.5.cloned.1.call-update) | async-done | bytes 524304 | tf_op jit(solution)/shard_map/reduce_scatter | solution.py:28
  373.4 1.8 convert_element_type.7
  (29 shorter events, 7.6 us)
Async XLA Ops:
  6.5 80.8 %copy-start = (bf16[64,2048]{1,0:T(8,128)(2,1)S(1)}, bf16[64,2048]{1,0:T(8,128)(2,1)}, u32[]{:S(2)}) copy-start(bf16[64,2048]{1,0:T(8,128)(2,1)} %param.6) | copy-start | bytes 786436
  6.5 226.6 %reduce-scatter.3.cloned.1.call-start = ((), (), s32[]{:S(2)}) async-start(), calls=%async_computation.2 | async-start | bytes 18923520 | tf_op jit(solution)/shard_map/reduce_scatter | solution.py:18
  6.5 12.6 %collective-permute-start = (bf16[64,2048]{1,0:T(8,128)(2,1)}, bf16[64,2048]{1,0:T(8,128)(2,1)S(1)}, u32[]{:S(2)}, u32[]{:S(2)}) collective-permute-start(bf16[64,2048]{1,0:T(8,128)(2,1)} %param.6), channel_id=1, source_target_pairs={{0,4},{4,8},{8,12},{12,16},{16,20},{20,24},{24,28},{28,0},{1,5},{5... | collective-permute-start | bytes 786440 | tf_op jit(solution)/shard_map/ppermute | solution.py:11
  19.2 10.2 %collective-permute-start.1 = (bf16[64,2048]{1,0:T(8,128)(2,1)S(1)}, bf16[64,2048]{1,0:T(8,128)(2,1)S(1)}, u32[]{:S(2)}, u32[]{:S(2)}) collective-permute-start(bf16[64,2048]{1,0:T(8,128)(2,1)S(1)} %collective-permute-done), channel_id=1, source_target_pairs={{0,4},{4,8},{8,12},{12,16},{16,20},{20,24},{24,28},{28,0},{1,5},{5... | collective-permute-start | bytes 786440 | tf_op jit(solution)/shard_map/ppermute | solution.py:11
  29.3 9.3 %collective-permute-start.2 = (bf16[64,2048]{1,0:T(8,128)(2,1)S(1)}, bf16[64,2048]{1,0:T(8,128)(2,1)S(1)}, u32[]{:S(2)}, u32[]{:S(2)}) collective-permute-start(bf16[64,2048]{1,0:T(8,128)(2,1)S(1)} %collective-permute-done.1), channel_id=1, source_target_pairs={{0,4},{4,8},{8,12},{12,16},{16,20},{20,24},{24,28},{28,0},{1,5},{5... | collective-permute-start | bytes 786440 | tf_op jit(solution)/shard_map/ppermute | solution.py:11
  38.6 9.1 %collective-permute-start.3 = (bf16[64,2048]{1,0:T(8,128)(2,1)S(1)}, bf16[64,2048]{1,0:T(8,128)(2,1)S(1)}, u32[]{:S(2)}, u32[]{:S(2)}) collective-permute-start(bf16[64,2048]{1,0:T(8,128)(2,1)S(1)} %collective-permute-done.2), channel_id=1, source_target_pairs={{0,4},{4,8},{8,12},{12,16},{16,20},{20,24},{24,28},{28,0},{1,5},{5... | collective-permute-start | bytes 786440 | tf_op jit(solution)/shard_map/ppermute | solution.py:11
  47.7 9.1 %collective-permute-start.4 = (bf16[64,2048]{1,0:T(8,128)(2,1)S(1)}, bf16[64,2048]{1,0:T(8,128)(2,1)S(1)}, u32[]{:S(2)}, u32[]{:S(2)}) collective-permute-start(bf16[64,2048]{1,0:T(8,128)(2,1)S(1)} %collective-permute-done.3), channel_id=1, source_target_pairs={{0,4},{4,8},{8,12},{12,16},{16,20},{20,24},{24,28},{28,0},{1,5},{5... | collective-permute-start | bytes 786440 | tf_op jit(solution)/shard_map/ppermute | solution.py:11
  56.8 9.7 %collective-permute-start.5 = (bf16[64,2048]{1,0:T(8,128)(2,1)S(1)}, bf16[64,2048]{1,0:T(8,128)(2,1)S(1)}, u32[]{:S(2)}, u32[]{:S(2)}) collective-permute-start(bf16[64,2048]{1,0:T(8,128)(2,1)S(1)} %collective-permute-done.4), channel_id=1, source_target_pairs={{0,4},{4,8},{8,12},{12,16},{16,20},{20,24},{24,28},{28,0},{1,5},{5... | collective-permute-start | bytes 786440 | tf_op jit(solution)/shard_map/ppermute | solution.py:11
  66.5 9.1 %collective-permute-start.6 = (bf16[64,2048]{1,0:T(8,128)(2,1)S(1)}, bf16[64,2048]{1,0:T(8,128)(2,1)S(1)}, u32[]{:S(2)}, u32[]{:S(2)}) collective-permute-start(bf16[64,2048]{1,0:T(8,128)(2,1)S(1)} %collective-permute-done.5), channel_id=1, source_target_pairs={{0,4},{4,8},{8,12},{12,16},{16,20},{20,24},{24,28},{28,0},{1,5},{5... | collective-permute-start | bytes 786440 | tf_op jit(solution)/shard_map/ppermute | solution.py:11
  123.0 0.9 copy-start.1
  123.0 147.7 %copy-start.2 = (f32[2048]{0:T(1024)S(1)}, f32[2048]{0:T(1024)}, u32[]{:S(2)}) copy-start(f32[2048]{0:T(1024)} %param.11) | copy-start | bytes 24580
  123.0 147.7 %all-gather.2.cloned.1.call-start = ((), (), s32[]{:S(2)}) async-start(), calls=%async_computation.3 | async-start | bytes 4730880 | tf_op jit(solution)/shard_map/all_gather | solution.py:27
  237.9 135.4 %reduce-scatter.5.cloned.1.call-start = ((), (), s32[]{:S(2)}) async-start(), calls=%async_computation.4 | async-start | bytes 4718592 | tf_op jit(solution)/shard_map/reduce_scatter | solution.py:28
Sparse Core Ops, SparseCore 0:
  123.1 109.9 reduce-scatter.2
  238.1 32.6 all-gather.1
  285.0 88.3 reduce-scatter.4
